TPU v7x, 32 devices: a whole 2x2x4 slice. The times are simulated.
32 devices in a mesh: panel: 8 (over y, x, core), samp: 4 (over z).
Axes of the slice: x: 2, y: 2, z: 4, core: 2. Of those that a mesh axis runs over, the one named last changes fastest.
Arguments:
- called_allele_tallies: int32 [2048, 1024], P('samp'), may hold values from 0 to 2
- presence_flags: int32 [2048, 1024], P('samp'), may hold values 0 or 1
- reference_panel_strands: int32 [16384, 1024], P('panel'), may hold values from 0 to 1
- softmax_sharpness: float32 [2048], P('samp'), may hold values from 0.02 to 4
- trait_measurements: float32 [2048], P('samp'), may hold values from -8 to 8
- cohort_membership: int32 [2048], P('samp'), may hold values from 0 to 7, as said below
Outputs:
- dosage_out: bfloat16 [2048, 1024], P('samp', 'panel')
- zscore: float32 [1024], P('panel')
Inputs may be any that keep to these rules, and one draw needn't show every extreme that they name: `cohort_membership`: every group id from 0 to 7 occurs.
All inputs are finite; a program needn't handle non-finite values. No bound on the sum of `presence_flags` on one device may be relied on, other than what follows from the above.
Results may differ from a plain program's by a relative error of at most 0.0055.
Values sent between devices are 32-bit elements; how exact they have to be, the bound alone decides.
A program may use at most 64 MiB of HBM per device.

v0:
```python
import jax
import jax.numpy as jnp
from jax import lax
from jax.sharding import PartitionSpec as P

GROUPS = 8


log_two = 0.6931471805599453


def on_device(
    called_allele_tallies,
    presence_flags,
    reference_panel_strands,
    softmax_sharpness,
    trait_measurements,
    cohort_membership,
):
    panel_count = lax.axis_size("panel")
    sample_rows, variants = called_allele_tallies.shape
    local_haps = reference_panel_strands.shape[0]
    hap_float = reference_panel_strands.astype(jnp.float32)
    allele_counts = lax.psum(jnp.sum(hap_float, axis=0), "panel")
    allele_freq = allele_counts / float(local_haps * panel_count)
    geno_float = called_allele_tallies.astype(jnp.float32)
    observed_f = presence_flags.astype(jnp.float32)
    demeaned_expected_count = (observed_f * (geno_float - 2.0 * allele_freq[None, :])).astype(
        jnp.bfloat16
    )
    tile_first_entry = jnp.sum(
        demeaned_expected_count.astype(jnp.float32) * allele_freq[None, :], axis=1
    )
    hap_bf = reference_panel_strands.astype(jnp.bfloat16)
    raw_efficient_statistic = lax.dot_general(
        demeaned_expected_count,
        hap_bf,
        (((1,), (1,)), ((), ())),
        preferred_element_type=jnp.float32,
    )
    panel_match_energies = softmax_sharpness[:, None] * (
        raw_efficient_statistic - tile_first_entry[:, None]
    )
    local_steps = jnp.ceil(jnp.max(panel_match_energies, axis=1) / log_two)
    share = variants // panel_count
    first_column = lax.axis_index("panel") * share
    peak_steps = lax.pmax(local_steps, "panel")
    weights = jnp.exp(panel_match_energies - log_two * peak_steps[:, None])
    weight_total = lax.psum(jnp.sum(weights, axis=1), "panel")
    partial_dose = 2.0 * jnp.dot(
        weights.astype(jnp.bfloat16), hap_bf, preferred_element_type=jnp.float32
    )
    own_dose = lax.psum_scatter(partial_dose, "panel", scatter_dimension=1, tiled=True)
    expected_allele_count = own_dose / weight_total[:, None]
    own_geno = lax.dynamic_slice_in_dim(geno_float, first_column, share, 1)
    own_observed = lax.dynamic_slice_in_dim(presence_flags, first_column, share, 1)
    dosage = jnp.where(own_observed == 1, own_geno, expected_allele_count)
    dosage_out = dosage.astype(jnp.bfloat16)
    member = (cohort_membership[:, None] == jnp.arange(GROUPS, dtype=jnp.int32)[None, :]).astype(
        jnp.float32
    )
    group_sum_local = jnp.dot(trait_measurements, member, precision=lax.Precision.HIGHEST)
    group_count_local = jnp.sum(member, axis=0)
    dose_sum_local = jnp.sum(dosage, axis=0)
    dose_square_local = jnp.sum(dosage * dosage, axis=0)
    all_samples = float(sample_rows * lax.axis_size("samp"))
    group_sum, group_count = lax.psum((group_sum_local, group_count_local), "samp")
    group_mean = group_sum / group_count
    resid = trait_measurements - jnp.dot(member, group_mean, precision=lax.Precision.HIGHEST)
    local_score = jnp.dot(resid, dosage, precision=lax.Precision.HIGHEST)
    score_u, dose_sum, dose_square, resid_square = lax.psum(
        (local_score, dose_sum_local, dose_square_local, jnp.sum(resid * resid)), "samp"
    )
    sigma = resid_square / (all_samples - GROUPS)
    dose_mean = dose_sum / all_samples
    spread = dose_square / all_samples - dose_mean * dose_mean
    zscore = score_u / jnp.sqrt(sigma * all_samples * (spread + 1e-05))
    return (dosage_out, zscore)


def solution(mesh):
    return jax.shard_map(
        on_device,
        mesh=mesh,
        in_specs=(
            P("samp", None),
            P("samp", None),
            P("panel", None),
            P("samp"),
            P("samp"),
            P("samp"),
        ),
        out_specs=(P("samp", "panel"), P("panel")),
        check_vma=False,
    )
```

profile of v0, /device:TPU:0, one launch (start us, length us, event | category | flops | bytes accessed | tf_op | source)
XLA Modules:
  0.0 120.0 jit_solution(17392454087837415897)
XLA Ops:
  7.2 0.0 copy-start
  7.2 0.0 reduce-scatter.2.cloned.1.call-start
  7.2 4.2 %convert_reduce_fusion = f32[1024]{0:T(1024)S(1)} fusion(s32[2048,1024]{1,0:T(8,128)} %param.8), kind=kLoop, calls=%fused_computation | loop fusion | flops 4193280 | bytes 8392704 | tf_op jit(solution)/shard_map/reduce_sum | solution.py:24
  11.4 0.0 copy-start.1
  11.4 15.2 %psum.56 = f32[1024]{0:T(1024)S(1)} all-reduce(f32[1024]{0:T(1024)S(1)} %convert_reduce_fusion), channel_id=1, replica_groups=mesh['panel'=8,'samp'=4] {'panel'}, use_global_device_ids=true, to_apply=%region_1.0 | all-reduce | flops 1024 | bytes 8192 | tf_op jit(solution)/shard_map/psum | solution.py:24
  26.5 0.0 copy-done
  26.6 2.1 %multiply_reduce_fusion = (f32[512]{0:T(512)S(1)}, bf16[512,1024]{1,0:T(8,128)(2,1)S(1)}) fusion(f32[1024]{0:T(1024)S(1)} %get-tuple-element.16, f32[1024]{0:T(1024)S(1)} %get-tuple-element.15, s32[512,1024]{1,0:T(8,128)S(1)} %copy-done, s32[512,1024]{1,0:T(8,128)} %param.7), kind=kLoop, calls=%fused_computation.9 | loop fusion | flops 4193792 | bytes 5253120 | tf_op jit(solution)/shard_map/reduce_sum | solution.py:31
  28.7 0.0 copy-done.1
  28.7 7.7 %fusion = (f32[512]{0:T(512)S(1)}, f32[512,2048]{1,0:T(8,128)}) fusion(f32[512]{0:T(512)S(1)} %get-tuple-element.13, f32[512]{0:T(512)S(1)} %copy-done.1, bf16[512,1024]{1,0:T(8,128)(2,1)S(1)} %get-tuple-element.14, s32[2048,1024]{1,0:T(8,128)} %param.8), kind=kOutput, calls=%fused_computation.3 | convolution fusion | flops 2152726016 | bytes 13637632 | tf_op jit(solution)/shard_map/dot_general | solution.py:35
  36.4 11.8 %pmax.7 = f32[512]{0:T(512)S(1)} all-reduce(f32[512]{0:T(512)S(1)} %multiply_ceil_fusion), channel_id=1, replica_groups=mesh['panel'=8,'samp'=4] {'panel'}, use_global_device_ids=true, to_apply=%region_4.0 | all-reduce | flops 512 | bytes 4096 | tf_op jit(solution)/shard_map/pmax | solution.py:47
  48.2 0.0 copy-start.2
  48.2 0.0 copy-start.3
  48.2 8.5 %fusion.11 = f32[512,1024]{1,0:T(8,128)} fusion(s32[2048,1024]{1,0:T(8,128)} %param.8, f32[512,2048]{1,0:T(8,128)} %get-tuple-element.18, f32[512]{0:T(512)S(1)} %broadcast_multiply_fusion.2, f32[512]{0:T(512)S(1)} %get-tuple-element.13, f32[512]{0:T(512)S(1)} %copy-done.1), kind=kOutput, calls=%fused_computation.15 | convolution fusion | flops 2154299392 | bytes 14686208 | tf_op jit(solution)/shard_map/dot_general | solution.py:50
  56.7 0.0 reduce-scatter.2.cloned.1.call-update
  56.7 0.0 copy-done.2
  56.7 0.0 copy-done.3
  56.7 0.1 convolution_bitcast_fusion.1
  56.9 0.1 convert_reduce_fusion.1
  57.0 12.0 %all-reduce.1 = (f32[8]{0:T(128)S(1)}, f32[8]{0:T(128)S(1)}) all-reduce(f32[8]{0:T(128)S(1)} %convolution_bitcast_fusion.1, f32[8]{0:T(128)S(1)} %convert_reduce_fusion.1), channel_id=1, replica_groups=mesh['panel'=8,'samp'=4] {'samp'}, use_global_device_ids=true, to_apply=%region_8.9 | all-reduce | flops 16 | bytes 128 | tf_op jit(solution)/shard_map/psum | solution.py:67
  69.0 1.5 %convert_element_type.27 = f32[512,1024]{1,0:T(8,128)} convert(s32[512,1024]{1,0:T(8,128)S(1)} %copy-done) | non-fusion elementwise | flops 524288 | bytes 4194304 | tf_op jit(solution)/shard_map/convert_element_type | solution.py:26
  70.5 3.1 %fusion.1 = f32[512]{0:T(512)S(1)} fusion(f32[512,2048]{1,0:T(8,128)} %get-tuple-element.18, f32[512]{0:T(512)S(1)} %broadcast_multiply_fusion.2, f32[512]{0:T(512)S(1)} %get-tuple-element.13, f32[512]{0:T(512)S(1)} %copy-done.1), kind=kLoop, calls=%fused_computation.4 | loop fusion | flops 4193792 | bytes 4202496 | tf_op jit(solution)/shard_map/reduce_sum | solution.py:49
  73.7 12.3 %psum.57 = f32[512]{0:T(512)S(1)} all-reduce(f32[512]{0:T(512)S(1)} %fusion.1), channel_id=1, replica_groups=mesh['panel'=8,'samp'=4] {'panel'}, use_global_device_ids=true, to_apply=%region_7.0 | all-reduce | flops 512 | bytes 4096 | tf_op jit(solution)/shard_map/psum | solution.py:49
  85.9 0.1 fusion.16
  86.1 0.6 multiply_reduce_fusion.2
  86.7 10.8 %reduce-scatter.2.cloned.1.call-done = f32[512,128]{1,0:T(8,128)} async-done(((f32[512,1024]{1,0:T(8,128)}), f32[512,128]{1,0:T(8,128)}) %reduce-scatter.2.cloned.1.call-update) | async-done | bytes 262160 | tf_op jit(solution)/shard_map/reduce_scatter | solution.py:53
  97.4 1.3 %multiply_reduce_fusion.1 = (f32[128]{0:T(128)S(1)}, f32[128]{0:T(128)S(1)}, f32[512,128]{1,0:T(8,128)S(1)}) fusion(f32[512,128]{1,0:T(8,128)} %reduce-scatter.2.cloned.1.call-done, f32[512]{0:T(512)S(1)} %psum.57, f32[512,1024]{1,0:T(8,128)} %convert_element_type.27, s32[]{:T(128)S(6)} %select_n.8, s32[512,1024]{1,0:T(8,128)} %param.7), kind=kLoop, calls=%fused_computation.18 | loop fusion | flops 392960 | bytes 1051652 | tf_op jit(solution)/shard_map/reduce_sum | solution.py:65
  98.7 0.7 convert_element_type.34
  99.4 0.2 convolution_bitcast_fusion
  99.6 12.3 %all-reduce = (f32[128]{0:T(128)S(1)}, f32[128]{0:T(128)S(1)}, f32[128]{0:T(128)S(1)}, f32[]{:T(128)}) all-reduce(f32[128]{0:T(128)S(1)} %convolution_bitcast_fusion, f32[128]{0:T(128)S(1)} %get-tuple-element.3, f32[128]{0:T(128)S(1)} %get-tuple-element.2, f32[]{:T(128)} %get-tuple-element.10), channel_id=1, replica_groups=mesh['panel'=8,'samp'=4] {'samp'}, use_global_device_ids=true, to_apply=%region_11.12 | all-reduce | flops 385 | bytes 3080 | tf_op jit(solution)/shard_map/psum | solution.py:71
  112.6 0.5 rsqrt_multiply_fusion
  (3 shorter events, 0.0 us)
Async XLA Ops:
  7.2 19.4 %copy-start = (s32[512,1024]{1,0:T(8,128)S(1)}, s32[512,1024]{1,0:T(8,128)}, u32[]{:S(2)}) copy-start(s32[512,1024]{1,0:T(8,128)} %param.6) | copy-start | bytes 6291460
  7.2 90.2 %reduce-scatter.2.cloned.1.call-start = ((), (), s32[]{:S(2)}) async-start(), calls=%async_computation.1 | async-start | bytes 2359296 | tf_op jit(solution)/shard_map/reduce_scatter | solution.py:53
  11.4 17.3 %copy-start.1 = (f32[512]{0:T(512)S(1)}, f32[512]{0:T(512)}, u32[]{:S(2)}) copy-start(f32[512]{0:T(512)} %param.9) | copy-start | bytes 6148
  48.2 8.5 %copy-start.2 = (s32[512]{0:T(512)S(1)}, s32[512]{0:T(512)}, u32[]{:S(2)}) copy-start(s32[512]{0:T(512)} %param.11) | copy-start | bytes 6148
  48.2 8.5 %copy-start.3 = (f32[512]{0:T(512)S(1)}, f32[512]{0:T(512)}, u32[]{:S(2)}) copy-start(f32[512]{0:T(512)} %param.10) | copy-start | bytes 6148
Sparse Core Ops, SparseCore 0:
  56.8 40.5 reduce-scatter.1
where the time goes:
time: 120 us
  blocking collectives  63.6 us (53%)
  matrix products  16.7 us (14%)
  between operations  14.7 us (12%)
  other arithmetic  14.2 us (12%)
  waiting for transfers between devices  10.8 us (9%)
    psum x1, blocking collectives, on_device(): allele_counts = lax.psum(jnp.sum(hap_float, axis=0), 'panel')  15.2 us
    psum x1, blocking collectives, on_device(): lax.psum((local_score, dose_sum_local, dose_square_local, jnp.sum(resid *...  12.3 us
    psum x1, blocking collectives, on_device(): weight_total = lax.psum(jnp.sum(weights, axis=1), 'panel')  12.3 us
    psum x1, blocking collectives, on_device(): lax.psum((group_sum_local, group_count_local), 'samp')  12 us
    pmax x1, blocking collectives, on_device(): peak_steps = lax.pmax(local_steps, 'panel')  11.8 us
    reduce_scatter x1, waiting for transfers between devices, on_device(): lax.psum_scatter(partial_dose, 'panel', scatter_dimension=1, tiled=True)  10.8 us
    dot_general x1, matrix products, on_device(): jnp.dot(weights.astype(jnp.bfloat16), hap_bf, preferred_element_type=jnp....  8.46 us
    dot_general x1, matrix products, on_device(): lax.dot_general(demeaned_expected_count, hap_bf, (((1,), (1,)), ((), ()))...  7.74 us
  transfers between devices with their start and end apart: 1, of which 1 were waited for; matrix products, arithmetic and copies ran while one was open for 5% of the time, Pallas kernels for 0%

commit v1 on v0

--- a/solution.py
+++ b/solution.py
@@ -1,6 +1,10 @@
+import functools
+
 import jax
 import jax.numpy as jnp
 from jax import lax
+from jax.experimental import pallas as pl
+from jax.experimental.pallas import tpu as pltpu
 from jax.sharding import PartitionSpec as P
 
 GROUPS = 8
@@ -78,9 +82,468 @@
     return (dosage_out, zscore)
 
 
+MESH = pl.DeviceIdType.MESH
+LANES = 128
+HAP_TILE = 256
+ROWS = 32
+VMEM_BYTES = 60 * 1024 * 1024
+
+
+def lane_copies(row):
+    blocks = [
+        jnp.broadcast_to(row[:, k : k + LANES], (LANES, LANES)).T
+        for k in range(0, row.shape[1], LANES)
+    ]
+    return jnp.concatenate(blocks, axis=0)
+
+
+def as_row(column):
+    blocks = [
+        jnp.broadcast_to(column[k : k + LANES], (LANES, LANES)).T[0:1]
+        for k in range(0, column.shape[0], LANES)
+    ]
+    return jnp.concatenate(blocks, axis=1)
+
+
+def fused(
+    panel_count,
+    samp_count,
+    tallies_hbm,
+    flags_hbm,
+    strands_hbm,
+    sharp_ref,
+    trait_ref,
+    cohort_ref,
+    dosage_ref,
+    zscore_ref,
+    strands_ref,
+    hap_ref,
+    tallies_ref,
+    flags_ref,
+    centred_ref,
+    logits_ref,
+    weights_ref,
+    counts_ref,
+    peaks_ref,
+    totals_ref,
+    groups_ref,
+    stats_ref,
+    sharp_col,
+    offset_col,
+    steps_col,
+    run_ref,
+    part_ref,
+    sib_ref,
+    out_ref,
+    in_ref,
+    strand_sems,
+    load_sems,
+    count_send,
+    count_recv,
+    peak_send,
+    peak_recv,
+    total_send,
+    total_recv,
+    group_send,
+    group_recv,
+    stat_send,
+    stat_recv,
+    sib_send,
+    sib_recv,
+    hop_send,
+    hop_recv,
+):
+    me = lax.axis_index("panel")
+    depth = lax.axis_index("samp")
+    samples, variants = tallies_ref.shape
+    haps = strands_ref.shape[0]
+    pieces = haps // HAP_TILE
+    core = me % 2
+    x = (me // 2) % 2
+    y = me // 4
+    sibling = me + 1 - 2 * core
+    x_peer = me + 2 - 4 * x
+    y_peer = me + 4 - 8 * y
+    first_peer = x_peer + core * (y_peer - x_peer)
+    second_peer = y_peer + core * (x_peer - y_peer)
+
+    def strand_load(i):
+        rows = pl.ds(i * HAP_TILE, HAP_TILE)
+        return pltpu.make_async_copy(
+            strands_hbm.at[rows], strands_ref.at[rows], strand_sems.at[i]
+        )
+
+    for i in range(pieces):
+        strand_load(i).start()
+    flag_load = pltpu.make_async_copy(flags_hbm, flags_ref, load_sems.at[0])
+    tally_load = pltpu.make_async_copy(tallies_hbm, tallies_ref, load_sems.at[1])
+    flag_load.start()
+    tally_load.start()
+
+    barrier = pltpu.get_barrier_semaphore()
+    for d in range(1, panel_count):
+        pl.semaphore_signal(
+            barrier, inc=1, device_id={"panel": (me + d) % panel_count}, device_id_type=MESH
+        )
+    for d in range(1, samp_count):
+        pl.semaphore_signal(
+            barrier, inc=1, device_id={"samp": (depth + d) % samp_count}, device_id_type=MESH
+        )
+    pl.semaphore_wait(barrier, panel_count + samp_count - 2)
+
+    def share_out(ref, send, recv, axis, count, mine):
+        copies = []
+        for d in range(1, count):
+            copy = pltpu.make_async_remote_copy(
+                src_ref=ref.at[mine],
+                dst_ref=ref.at[mine],
+                send_sem=send.at[d - 1],
+                recv_sem=recv.at[d - 1],
+                device_id={axis: (mine + d) % count},
+                device_id_type=MESH,
+            )
+            copy.start()
+            copies.append(copy)
+
+        def arrive():
+            for d in range(1, count):
+                slot = (mine + count - d) % count
+                pltpu.make_async_remote_copy(
+                    src_ref=ref.at[slot],
+                    dst_ref=ref.at[slot],
+                    send_sem=send.at[d - 1],
+                    recv_sem=recv.at[d - 1],
+                    device_id={axis: (mine + d) % count},
+                    device_id_type=MESH,
+                ).wait_recv()
+
+        def sent():
+            for copy in copies:
+                copy.wait_send()
+
+        return arrive, sent
+
+    trait = trait_ref[...]
+    member = (
+        lax.broadcasted_iota(jnp.int32, (GROUPS, samples), 0)
+        == jnp.broadcast_to(cohort_ref[...], (GROUPS, samples))
+    ).astype(jnp.float32)
+    group_sum = jnp.sum(member * trait, axis=1, keepdims=True)
+    group_count = jnp.sum(member, axis=1, keepdims=True)
+    lane = lax.broadcasted_iota(jnp.int32, (GROUPS, LANES), 1)
+    groups_ref[depth] = jnp.where(lane == 0, group_sum, group_count)
+    groups_arrive, groups_sent = share_out(
+        groups_ref, group_send, group_recv, "samp", samp_count, depth
+    )
+    sharp_col[...] = lane_copies(sharp_ref[...])
+
+    def convert_piece(i, acc):
+        strand_load(i).wait()
+
+        def convert_rows(r, acc):
+            start = pl.multiple_of(i * HAP_TILE + r * ROWS, ROWS)
+            strands = strands_ref[pl.ds(start, ROWS)]
+            hap_ref[pl.ds(start, ROWS)] = strands.astype(jnp.float32).astype(jnp.bfloat16)
+            for k in range(0, ROWS, 8):
+                acc = acc + strands[k : k + 8]
+            return acc
+
+        return lax.fori_loop(0, HAP_TILE // ROWS, convert_rows, acc)
+
+    acc = lax.fori_loop(0, pieces, convert_piece, jnp.zeros((8, variants), jnp.int32))
+    counts_ref[me] = jnp.sum(acc.astype(jnp.float32), axis=0, keepdims=True)
+    counts_arrive, counts_sent = share_out(
+        counts_ref, count_send, count_recv, "panel", panel_count, me
+    )
+    flag_load.wait()
+    tally_load.wait()
+
+    groups_arrive()
+    group_all = groups_ref[0]
+    for k in range(1, samp_count):
+        group_all = group_all + groups_ref[k]
+    group_mean = group_all[:, 0:1] / group_all[:, 1:2]
+    resid = trait - jnp.sum(member * group_mean, axis=0, keepdims=True)
+    resid_square = jnp.sum(resid * resid, axis=1, keepdims=True)
+
+    counts_arrive()
+    counts = counts_ref[0]
+    for k in range(1, panel_count):
+        counts = counts + counts_ref[k]
+    freq = counts / float(haps * panel_count)
+
+    def centre(r, _):
+        rows = pl.ds(pl.multiple_of(r * ROWS, ROWS), ROWS)
+        seen = flags_ref[rows].astype(jnp.float32)
+        geno = tallies_ref[rows].astype(jnp.float32)
+        centred = (seen * (geno - 2.0 * freq)).astype(jnp.bfloat16)
+        centred_ref[rows] = centred
+        offset = jnp.sum(centred.astype(jnp.float32) * freq, axis=1, keepdims=True)
+        offset_col[rows] = jnp.broadcast_to(offset, (ROWS, LANES))
+        return 0
+
+    lax.fori_loop(0, samples // ROWS, centre, 0)
+
+    run_ref[...] = jnp.full_like(run_ref, -jnp.inf)
+
+    def match(i, _):
+        hap = hap_ref[pl.ds(pl.multiple_of(i * HAP_TILE, HAP_TILE), HAP_TILE)]
+        raw = lax.dot_general(
+            centred_ref[...], hap, (((1,), (1,)), ((), ())), preferred_element_type=jnp.float32
+        )
+        sharp = sharp_col[...]
+        offset = offset_col[...]
+        best = run_ref[...]
+        for k in range(0, HAP_TILE, LANES):
+            energy = sharp * (raw[:, k : k + LANES] - offset)
+            logits_ref[i, :, k : k + LANES] = energy
+            best = jnp.maximum(best, energy)
+        run_ref[...] = best
+        return 0
+
+    lax.fori_loop(0, pieces, match, 0)
+    steps = jnp.ceil(jnp.max(run_ref[...], axis=1, keepdims=True) / log_two)
+    steps_col[...] = jnp.broadcast_to(steps, steps_col.shape)
+    local_steps = as_row(steps)
+    peaks_ref[me] = local_steps
+    peaks_arrive, peaks_sent = share_out(peaks_ref, peak_send, peak_recv, "panel", panel_count, me)
+
+    run_ref[...] = jnp.zeros_like(run_ref)
+
+    def weigh(r, _):
+        rows = pl.ds(pl.multiple_of(r * ROWS, ROWS), ROWS)
+        shift = log_two * steps_col[rows]
+        total = jnp.zeros((ROWS, LANES), jnp.float32)
+        for i in range(pieces):
+            for k in range(0, HAP_TILE, LANES):
+                weight = jnp.exp(logits_ref[i, rows, k : k + LANES] - shift)
+                total = total + weight
+                first = i * HAP_TILE + k
+                weights_ref[rows, first : first + LANES] = weight.astype(jnp.bfloat16)
+        run_ref[rows] = total
+        return 0
+
+    lax.fori_loop(0, samples // ROWS, weigh, 0)
+    totals_ref[me] = as_row(jnp.sum(run_ref[...], axis=1, keepdims=True))
+    totals_arrive, totals_sent = share_out(
+        totals_ref, total_send, total_recv, "panel", panel_count, me
+    )
+
+    def allele_sums(chip):
+        columns = pl.ds(pl.multiple_of(chip * 2 * LANES, 2 * LANES), 2 * LANES)
+        return jnp.dot(
+            weights_ref[...], hap_ref[:, columns], preferred_element_type=jnp.float32
+        )
+
+    def hand_over(i):
+        copy = pltpu.make_async_remote_copy(
+            src_ref=part_ref.at[i, 1 - core],
+            dst_ref=sib_ref.at[i],
+            send_sem=sib_send.at[i],
+            recv_sem=sib_recv.at[i],
+            device_id={"panel": sibling},
+            device_id_type=MESH,
+        )
+        copy.start()
+        return copy
+
+    def hop(i, peer):
+        copy = pltpu.make_async_remote_copy(
+            src_ref=out_ref.at[i],
+            dst_ref=in_ref.at[i],
+            send_sem=hop_send.at[i],
+            recv_sem=hop_recv.at[i],
+            device_id={"panel": peer},
+            device_id_type=MESH,
+        )
+        copy.start()
+        return copy
+
+    diag_chip = (1 - y) * 2 + 1 - x
+    x_chip = y * 2 + 1 - x
+    y_chip = (1 - y) * 2 + x
+    own_chip = y * 2 + x
+    handed = []
+    scale = None
+    hops = []
+    for i, chip in enumerate((diag_chip, x_chip, y_chip, own_chip)):
+        part = allele_sums(chip)
+        if i == 0:
+            peaks_arrive()
+            top = peaks_ref[0]
+            for k in range(1, panel_count):
+                top = jnp.maximum(top, peaks_ref[k])
+            steps_col[...] = lane_copies(jnp.exp2(local_steps - top))
+        scale = steps_col[...]
+        part_ref[i, 0] = scale * part[:, :LANES]
+        part_ref[i, 1] = scale * part[:, LANES:]
+        handed.append(hand_over(i))
+        if i == 1:
+            handed[0].wait_recv()
+            out_ref[0] = part_ref[0, core] + sib_ref[0]
+            hops.append(hop(0, first_peer))
+
+    near = 1 + core
+    far = 2 - core
+    handed[1].wait_recv()
+    handed[2].wait_recv()
+    out_ref[1] = part_ref[near, core] + sib_ref[near]
+    hops.append(hop(1, first_peer))
+    out_ref[2] = part_ref[far, core] + sib_ref[far]
+
+    totals_arrive()
+    weight_total = totals_ref[0] * jnp.exp2(peaks_ref[0] - top)
+    for k in range(1, panel_count):
+        weight_total = weight_total + totals_ref[k] * jnp.exp2(peaks_ref[k] - top)
+    sharp_col[...] = lane_copies(2.0 / weight_total)
+    offset_col[...] = lane_copies(resid)
+    handed[3].wait_recv()
+    run_ref[...] = part_ref[3, core] + sib_ref[3]
+
+    hops[0].wait_recv()
+    out_ref[2] = out_ref[2] + in_ref[0]
+    hops.append(hop(2, second_peer))
+    hops[1].wait_recv()
+    run_ref[...] = run_ref[...] + in_ref[1]
+    hops[2].wait_recv()
+
+    own = pl.ds(pl.multiple_of(me * LANES, LANES), LANES)
+
+    def finish(r, sums):
+        rows = pl.ds(pl.multiple_of(r * ROWS, ROWS), ROWS)
+        imputed = (run_ref[rows] + in_ref[2, rows]) * sharp_col[rows]
+        dosage = jnp.where(
+            flags_ref[rows, own] == 1, tallies_ref[rows, own].astype(jnp.float32), imputed
+        )
+        dosage_ref[rows] = dosage.astype(jnp.bfloat16)
+        score, dose, square = sums
+        weighted = offset_col[rows] * dosage
+        squared = dosage * dosage
+        for k in range(0, ROWS, 8):
+            score = score + weighted[k : k + 8]
+            dose = dose + dosage[k : k + 8]
+            square = square + squared[k : k + 8]
+        return score, dose, square
+
+    zero = jnp.zeros((8, LANES), jnp.float32)
+    sums = lax.fori_loop(0, samples // ROWS, finish, (zero, zero, zero))
+    line = lax.broadcasted_iota(jnp.int32, (8, LANES), 0)
+    score, dose, square = (jnp.sum(s, axis=0, keepdims=True) for s in sums)
+    stats_ref[depth] = jnp.where(
+        line == 0, score, jnp.where(line == 1, dose, jnp.where(line == 2, square, resid_square))
+    )
+    stats_arrive, stats_sent = share_out(
+        stats_ref, stat_send, stat_recv, "samp", samp_count, depth
+    )
+    stats_arrive()
+    stats = stats_ref[0]
+    for k in range(1, samp_count):
+        stats = stats + stats_ref[k]
+    all_samples = float(samples * samp_count)
+    sigma = stats[3:4] / (all_samples - GROUPS)
+    dose_mean = stats[1:2] / all_samples
+    spread = stats[2:3] / all_samples - dose_mean * dose_mean
+    zscore_ref[...] = stats[0:1] / jnp.sqrt(sigma * all_samples * (spread + 1e-05))
+
+    for sent in (groups_sent, counts_sent, peaks_sent, totals_sent, stats_sent):
+        sent()
+    for copy in handed + hops:
+        copy.wait_send()
+
+
+def fused_on_device(panel_count, samp_count, tallies, flags, strands, sharp, trait, cohort):
+    samples, variants = tallies.shape
+    haps = strands.shape[0]
+    f32, bf16, i32 = jnp.float32, jnp.bfloat16, jnp.int32
+    column = pltpu.VMEM((samples, LANES), f32)
+    peers = pltpu.SemaphoreType.DMA((panel_count - 1,))
+    levels = pltpu.SemaphoreType.DMA((samp_count - 1,))
+    anywhere = pl.BlockSpec(memory_space=pl.ANY)
+    local = pl.BlockSpec(memory_space=pltpu.VMEM)
+    dosage, zscore = pl.pallas_call(
+        functools.partial(fused, panel_count, samp_count),
+        out_shape=(
+            jax.ShapeDtypeStruct((samples, LANES), bf16),
+            jax.ShapeDtypeStruct((1, LANES), f32),
+        ),
+        in_specs=[anywhere] * 3 + [local] * 3,
+        out_specs=(local, local),
+        scratch_shapes=[
+            pltpu.VMEM((haps, variants), i32),
+            pltpu.VMEM((haps, variants), bf16),
+            pltpu.VMEM((samples, variants), i32),
+            pltpu.VMEM((samples, variants), i32),
+            pltpu.VMEM((samples, variants), bf16),
+            pltpu.VMEM((haps // HAP_TILE, samples, HAP_TILE), f32),
+            pltpu.VMEM((samples, haps), bf16),
+            pltpu.VMEM((panel_count, 1, variants), f32),
+            pltpu.VMEM((panel_count, 1, samples), f32),
+            pltpu.VMEM((panel_count, 1, samples), f32),
+            pltpu.VMEM((samp_count, GROUPS, LANES), f32),
+            pltpu.VMEM((samp_count, 8, LANES), f32),
+            column,
+            column,
+            column,
+            column,
+            pltpu.VMEM((4, 2, samples, LANES), f32),
+            pltpu.VMEM((4, samples, LANES), f32),
+            pltpu.VMEM((3, samples, LANES), f32),
+            pltpu.VMEM((3, samples, LANES), f32),
+            pltpu.SemaphoreType.DMA((haps // HAP_TILE,)),
+            pltpu.SemaphoreType.DMA((2,)),
+            peers,
+            peers,
+            peers,
+            peers,
+            peers,
+            peers,
+            levels,
+            levels,
+            levels,
+            levels,
+            pltpu.SemaphoreType.DMA((4,)),
+            pltpu.SemaphoreType.DMA((4,)),
+            pltpu.SemaphoreType.DMA((3,)),
+            pltpu.SemaphoreType.DMA((3,)),
+        ],
+        compiler_params=pltpu.CompilerParams(
+            collective_id=0, has_side_effects=True, vmem_limit_bytes=VMEM_BYTES
+        ),
+        name="impute",
+    )(
+        tallies,
+        flags,
+        strands,
+        sharp.reshape(1, samples),
+        trait.reshape(1, samples),
+        cohort.reshape(1, samples),
+    )
+    return dosage, zscore.reshape(LANES)
+
+
+def body_for(mesh):
+    panel_count, samp_count = mesh.shape["panel"], mesh.shape["samp"]
+
+    def body(tallies, flags, strands, sharp, trait, cohort):
+        samples, variants = tallies.shape
+        fits = (
+            panel_count == 2 * 2 * 2
+            and samp_count > 1
+            and variants == panel_count * LANES
+            and samples % LANES == 0
+            and strands.shape[0] % HAP_TILE == 0
+        )
+        args = (tallies, flags, strands, sharp, trait, cohort)
+        if fits:
+            return fused_on_device(panel_count, samp_count, *args)
+        return on_device(*args)
+
+    return body
+
+
 def solution(mesh):
     return jax.shard_map(
-        on_device,
+        body_for(mesh),
         mesh=mesh,
         in_specs=(
             P("samp", None),

time: 120 us -> 42 us (0.35)
  blocking collectives: 63.6 us -> 0 us
  Pallas kernels: 0 us -> 38.4 us
  matrix products: 16.7 us -> 0 us
  other arithmetic: 14.2 us -> 0 us
  between operations: 14.7 us -> 0.64 us
  waiting for transfers between devices: 10.8 us -> 0 us
  local copies, waits for them, and re-layouts: 0.02 us -> 2.74 us
    psum x4 -> x0, blocking collectives: 51.8 us -> none  [the longest x1 15.2 us: on_device(): allele_counts = lax.psum(jnp.sum(hap_float, axis=0), 'panel')]
    pallas_call x0 -> x1, Pallas kernels: none -> 38.4 us  [fused_on_device(): pl.pallas_call(functools.partial(fused, panel_count, samp_count), out_sha...]
    dot_general x5 -> x0, matrix products: 16.7 us -> none  [the longest x1 8.46 us: on_device(): jnp.dot(weights.astype(jnp.bfloat16), hap_bf, preferred_element_type=jnp....]
    pmax x1 -> x0, blocking collectives: 11.8 us -> none  [on_device(): peak_steps = lax.pmax(local_steps, 'panel')]
    reduce_sum x6 -> x0, other arithmetic: 11.4 us -> none  [the longest x1 4.16 us: on_device(): allele_counts = lax.psum(jnp.sum(hap_float, axis=0), 'panel')]
    reduce_scatter x1 -> x0, waiting for transfers between devices: 10.8 us -> none  [on_device(): lax.psum_scatter(partial_dose, 'panel', scatter_dimension=1, tiled=True)]
    unnamed x8 -> x2, local copies, waits for them, and re-layouts: 0.02 us -> 2.74 us
    convert_element_type x2 -> x0, other arithmetic: 2.18 us -> none  [the longest x1 1.51 us: on_device(): geno_float = called_allele_tallies.astype(jnp.float32)]
  transfers between devices with their start and end apart: 1 -> 0, of which waited for: 1 -> 0; matrix products, arithmetic and copies ran while one was open for 5% -> 0% of each run, Pallas kernels for 0% -> 0%
where the time goes in v1:
time: 42 us; the launch traced here: 41.8 us
  Pallas kernels  38.4 us (91%)
  local copies, waits for them, and re-layouts  2.74 us (7%)
  between operations  0.64 us (2%)
    pallas_call x1, Pallas kernels, fused_on_device(): pl.pallas_call(functools.partial(fused, panel_count, samp_count), out_sha...  38.4 us
    unnamed x2, local copies, waits for them, and re-layouts  2.74 us

profile of v1, /device:TPU:0, one launch (start us, length us, event | category | flops | bytes accessed | tf_op | source)
XLA Modules:
  0.0 41.8 jit_solution(17999492165240120845)
XLA Ops:
  0.6 38.4 %impute.1 = (bf16[512,128]{1,0:T(8,128)(2,1)}, f32[1,128]{1,0:T(1,128)}) custom-call(s32[512,1024]{1,0:T(8,128)} %tallies_hbm.1, s32[512,1024]{1,0:T(8,128)} %flags_hbm.1, s32[2048,1024]{1,0:T(8,128)} %strands_hbm.1, f32[1,512]{1,0:T(1,128)} %bitcast.4, f32[1,512]{1,0:T(1,128)} %bitcast.5, s32[1,512]{1,0:T(1,128)} %bitcast.6), custom_call_target="tpu_custom_call" | custom-call | tf_op jit(solution)/shard_map/impute/pallas_call | solution.py:463
  39.0 1.6 %copy.10 = bf16[512,128]{1,0:T(8,128)(2,1)} copy(bf16[512,128]{1,0:T(8,128)(2,1)} %get-tuple-element.8) | data formatting | bytes 262144
  40.6 1.2 %copy.11 = f32[128]{0:T(128)} copy(f32[128]{0:T(128)} %bitcast.7) | data formatting | bytes 1024

commit v2 on v1

--- a/solution.py
+++ b/solution.py
@@ -120,17 +120,21 @@
     hap_ref,
     tallies_ref,
     flags_ref,
+    code_ref,
     centred_ref,
     logits_ref,
     weights_ref,
     counts_ref,
     peaks_ref,
+    chip_peak_ref,
     totals_ref,
     groups_ref,
     stats_ref,
     sharp_col,
     offset_col,
     steps_col,
+    mine_col,
+    first_col,
     run_ref,
     part_ref,
     sib_ref,
@@ -177,8 +181,6 @@
         strand_load(i).start()
     flag_load = pltpu.make_async_copy(flags_hbm, flags_ref, load_sems.at[0])
     tally_load = pltpu.make_async_copy(tallies_hbm, tallies_ref, load_sems.at[1])
-    flag_load.start()
-    tally_load.start()
 
     barrier = pltpu.get_barrier_semaphore()
     for d in range(1, panel_count):
@@ -189,7 +191,6 @@
         pl.semaphore_signal(
             barrier, inc=1, device_id={"samp": (depth + d) % samp_count}, device_id_type=MESH
         )
-    pl.semaphore_wait(barrier, panel_count + samp_count - 2)
 
     def share_out(ref, send, recv, axis, count, mine):
         copies = []
@@ -223,6 +224,29 @@
 
         return arrive, sent
 
+    def convert_piece(i, acc):
+        strand_load(i).wait()
+
+        def convert_rows(r, acc):
+            start = pl.multiple_of(i * HAP_TILE + r * ROWS, ROWS)
+            strands = strands_ref[pl.ds(start, ROWS)]
+            hap_ref[pl.ds(start, ROWS)] = strands.astype(jnp.float32).astype(jnp.bfloat16)
+            for k in range(0, ROWS, 8):
+                acc = acc + strands[k : k + 8]
+            return acc
+
+        return lax.fori_loop(0, HAP_TILE // ROWS, convert_rows, acc)
+
+    early = pieces // 2
+    acc = lax.fori_loop(0, early, convert_piece, jnp.zeros((8, variants), jnp.int32))
+    flag_load.start()
+    tally_load.start()
+    acc = lax.fori_loop(early, pieces, convert_piece, acc)
+    pl.semaphore_wait(barrier, panel_count + samp_count - 2)
+    counts_ref[me] = jnp.sum(acc.astype(jnp.float32), axis=0, keepdims=True)
+    counts_arrive, counts_sent = share_out(
+        counts_ref, count_send, count_recv, "panel", panel_count, me
+    )
     trait = trait_ref[...]
     member = (
         lax.broadcasted_iota(jnp.int32, (GROUPS, samples), 0)
@@ -237,34 +261,16 @@
     )
     sharp_col[...] = lane_copies(sharp_ref[...])
 
-    def convert_piece(i, acc):
-        strand_load(i).wait()
-
-        def convert_rows(r, acc):
-            start = pl.multiple_of(i * HAP_TILE + r * ROWS, ROWS)
-            strands = strands_ref[pl.ds(start, ROWS)]
-            hap_ref[pl.ds(start, ROWS)] = strands.astype(jnp.float32).astype(jnp.bfloat16)
-            for k in range(0, ROWS, 8):
-                acc = acc + strands[k : k + 8]
-            return acc
-
-        return lax.fori_loop(0, HAP_TILE // ROWS, convert_rows, acc)
-
-    acc = lax.fori_loop(0, pieces, convert_piece, jnp.zeros((8, variants), jnp.int32))
-    counts_ref[me] = jnp.sum(acc.astype(jnp.float32), axis=0, keepdims=True)
-    counts_arrive, counts_sent = share_out(
-        counts_ref, count_send, count_recv, "panel", panel_count, me
-    )
     flag_load.wait()
     tally_load.wait()
 
-    groups_arrive()
-    group_all = groups_ref[0]
-    for k in range(1, samp_count):
-        group_all = group_all + groups_ref[k]
-    group_mean = group_all[:, 0:1] / group_all[:, 1:2]
-    resid = trait - jnp.sum(member * group_mean, axis=0, keepdims=True)
-    resid_square = jnp.sum(resid * resid, axis=1, keepdims=True)
+    def encode(r, _):
+        rows = pl.ds(pl.multiple_of(r * ROWS, ROWS), ROWS)
+        code = jnp.where(flags_ref[rows] == 1, tallies_ref[rows], -1)
+        code_ref[rows] = code.astype(jnp.float32)
+        return 0
+
+    lax.fori_loop(0, samples // ROWS, encode, 0)
 
     counts_arrive()
     counts = counts_ref[0]
@@ -272,22 +278,29 @@
         counts = counts + counts_ref[k]
     freq = counts / float(haps * panel_count)
 
+    twice = 2.0 * freq
+
     def centre(r, _):
         rows = pl.ds(pl.multiple_of(r * ROWS, ROWS), ROWS)
-        seen = flags_ref[rows].astype(jnp.float32)
-        geno = tallies_ref[rows].astype(jnp.float32)
-        centred = (seen * (geno - 2.0 * freq)).astype(jnp.bfloat16)
+        code = code_ref[rows]
+        centred = jnp.where(code >= 0.0, code - twice, 0.0).astype(jnp.bfloat16)
         centred_ref[rows] = centred
-        offset = jnp.sum(centred.astype(jnp.float32) * freq, axis=1, keepdims=True)
-        offset_col[rows] = jnp.broadcast_to(offset, (ROWS, LANES))
+        term = centred.astype(jnp.float32) * freq
+        offset = term[:, :LANES]
+        for k in range(LANES, variants, LANES):
+            offset = offset + term[:, k : k + LANES]
+        offset_col[rows] = offset
         return 0
 
     lax.fori_loop(0, samples // ROWS, centre, 0)
+    offset_col[...] = jnp.broadcast_to(
+        jnp.sum(offset_col[...], axis=1, keepdims=True), offset_col.shape
+    )
 
     run_ref[...] = jnp.full_like(run_ref, -jnp.inf)
 
     def match(i, _):
-        hap = hap_ref[pl.ds(pl.multiple_of(i * HAP_TILE, HAP_TILE), HAP_TILE)]
+        hap = hap_ref[i * HAP_TILE : (i + 1) * HAP_TILE]
         raw = lax.dot_general(
             centred_ref[...], hap, (((1,), (1,)), ((), ())), preferred_element_type=jnp.float32
         )
@@ -301,12 +314,24 @@
         run_ref[...] = best
         return 0
 
-    lax.fori_loop(0, pieces, match, 0)
+    for i in range(pieces):
+        match(i, 0)
     steps = jnp.ceil(jnp.max(run_ref[...], axis=1, keepdims=True) / log_two)
     steps_col[...] = jnp.broadcast_to(steps, steps_col.shape)
     local_steps = as_row(steps)
     peaks_ref[me] = local_steps
-    peaks_arrive, peaks_sent = share_out(peaks_ref, peak_send, peak_recv, "panel", panel_count, me)
+    sibling_peaks = pltpu.make_async_remote_copy(
+        src_ref=peaks_ref.at[me],
+        dst_ref=chip_peak_ref,
+        send_sem=sib_send.at[4],
+        recv_sem=sib_recv.at[4],
+        device_id={"panel": sibling},
+        device_id_type=MESH,
+    )
+    sibling_peaks.start()
+    peaks_arrive, peaks_sent = share_out(
+        peaks_ref, peak_send, peak_recv, "panel", panel_count, me
+    )
 
     run_ref[...] = jnp.zeros_like(run_ref)
 
@@ -331,8 +356,11 @@
 
     def allele_sums(chip):
         columns = pl.ds(pl.multiple_of(chip * 2 * LANES, 2 * LANES), 2 * LANES)
+        half = haps // 2
         return jnp.dot(
-            weights_ref[...], hap_ref[:, columns], preferred_element_type=jnp.float32
+            weights_ref[:, :half], hap_ref[:half, columns], preferred_element_type=jnp.float32
+        ) + jnp.dot(
+            weights_ref[:, half:], hap_ref[half:, columns], preferred_element_type=jnp.float32
         )
 
     def hand_over(i):
@@ -369,11 +397,9 @@
     for i, chip in enumerate((diag_chip, x_chip, y_chip, own_chip)):
         part = allele_sums(chip)
         if i == 0:
-            peaks_arrive()
-            top = peaks_ref[0]
-            for k in range(1, panel_count):
-                top = jnp.maximum(top, peaks_ref[k])
-            steps_col[...] = lane_copies(jnp.exp2(local_steps - top))
+            sibling_peaks.wait_recv()
+            chip_top = jnp.maximum(local_steps, chip_peak_ref[...])
+            steps_col[...] = lane_copies(jnp.exp2(local_steps - chip_top))
         scale = steps_col[...]
         part_ref[i, 0] = scale * part[:, :LANES]
         part_ref[i, 1] = scale * part[:, LANES:]
@@ -389,22 +415,36 @@
     handed[2].wait_recv()
     out_ref[1] = part_ref[near, core] + sib_ref[near]
     hops.append(hop(1, first_peer))
-    out_ref[2] = part_ref[far, core] + sib_ref[far]
-
+
+    peaks_arrive()
+    top = peaks_ref[0]
+    for k in range(1, panel_count):
+        top = jnp.maximum(top, peaks_ref[k])
+    first_top = jnp.maximum(peaks_ref[first_peer], peaks_ref[first_peer + 1 - 2 * core])
+    mine_col[...] = lane_copies(jnp.exp2(chip_top - top))
+    first_col[...] = lane_copies(jnp.exp2(first_top - top))
     totals_arrive()
     weight_total = totals_ref[0] * jnp.exp2(peaks_ref[0] - top)
     for k in range(1, panel_count):
         weight_total = weight_total + totals_ref[k] * jnp.exp2(peaks_ref[k] - top)
     sharp_col[...] = lane_copies(2.0 / weight_total)
+    groups_arrive()
+    group_all = groups_ref[0]
+    for k in range(1, samp_count):
+        group_all = group_all + groups_ref[k]
+    group_mean = group_all[:, 0:1] / group_all[:, 1:2]
+    resid = trait - jnp.sum(member * group_mean, axis=0, keepdims=True)
+    resid_square = jnp.sum(resid * resid, axis=1, keepdims=True)
     offset_col[...] = lane_copies(resid)
     handed[3].wait_recv()
-    run_ref[...] = part_ref[3, core] + sib_ref[3]
+    run_ref[...] = mine_col[...] * (part_ref[3, core] + sib_ref[3])
+    out_ref[2] = mine_col[...] * (part_ref[far, core] + sib_ref[far])
 
     hops[0].wait_recv()
-    out_ref[2] = out_ref[2] + in_ref[0]
+    out_ref[2] = out_ref[2] + first_col[...] * in_ref[0]
     hops.append(hop(2, second_peer))
     hops[1].wait_recv()
-    run_ref[...] = run_ref[...] + in_ref[1]
+    run_ref[...] = run_ref[...] + first_col[...] * in_ref[1]
     hops[2].wait_recv()
 
     own = pl.ds(pl.multiple_of(me * LANES, LANES), LANES)
@@ -447,8 +487,13 @@
 
     for sent in (groups_sent, counts_sent, peaks_sent, totals_sent, stats_sent):
         sent()
-    for copy in handed + hops:
+    for copy in [sibling_peaks] + handed + hops:
         copy.wait_send()
+
+
+def hand_out(dosage_in, zscore_in, dosage_out, zscore_out):
+    dosage_out[...] = dosage_in[...]
+    zscore_out[...] = zscore_in[...]
 
 
 def fused_on_device(panel_count, samp_count, tallies, flags, strands, sharp, trait, cohort):
@@ -473,14 +518,18 @@
             pltpu.VMEM((haps, variants), bf16),
             pltpu.VMEM((samples, variants), i32),
             pltpu.VMEM((samples, variants), i32),
+            pltpu.VMEM((samples, variants), f32),
             pltpu.VMEM((samples, variants), bf16),
             pltpu.VMEM((haps // HAP_TILE, samples, HAP_TILE), f32),
             pltpu.VMEM((samples, haps), bf16),
             pltpu.VMEM((panel_count, 1, variants), f32),
             pltpu.VMEM((panel_count, 1, samples), f32),
+            pltpu.VMEM((1, samples), f32),
             pltpu.VMEM((panel_count, 1, samples), f32),
             pltpu.VMEM((samp_count, GROUPS, LANES), f32),
             pltpu.VMEM((samp_count, 8, LANES), f32),
+            column,
+            column,
             column,
             column,
             column,
@@ -501,8 +550,8 @@
             levels,
             levels,
             levels,
-            pltpu.SemaphoreType.DMA((4,)),
-            pltpu.SemaphoreType.DMA((4,)),
+            pltpu.SemaphoreType.DMA((5,)),
+            pltpu.SemaphoreType.DMA((5,)),
             pltpu.SemaphoreType.DMA((3,)),
             pltpu.SemaphoreType.DMA((3,)),
         ],
@@ -518,6 +567,16 @@
         trait.reshape(1, samples),
         cohort.reshape(1, samples),
     )
+    dosage, zscore = pl.pallas_call(
+        hand_out,
+        out_shape=(
+            jax.ShapeDtypeStruct((samples, LANES), bf16),
+            jax.ShapeDtypeStruct((1, LANES), f32),
+        ),
+        in_specs=[local, local],
+        out_specs=(local, local),
+        name="hand_out",
+    )(dosage, zscore)
     return dosage, zscore.reshape(LANES)
 
 

time: 42 us -> 36.1 us (0.86)
  Pallas kernels: 38.4 us -> 35.2 us
  local copies, waits for them, and re-layouts: 2.74 us -> 0 us
    pallas_call x1, Pallas kernels: 38.4 us -> 33.7 us  [fused_on_device(): pl.pallas_call(functools.partial(fused, panel_count, samp_count), out_sha...]
    unnamed x2 -> x0, local copies, waits for them, and re-layouts: 2.74 us -> none
    pallas_call x0 -> x1, Pallas kernels: none -> 1.57 us  [fused_on_device(): pl.pallas_call(hand_out, out_shape=(jax.ShapeDtypeStruct((samples, LANES)...]
where the time goes in v2:
time: 36.1 us; the launch traced here: 35.9 us
  Pallas kernels  35.2 us (98%)
  between operations  0.64 us (2%)
    pallas_call x1, Pallas kernels, fused_on_device(): pl.pallas_call(functools.partial(fused, panel_count, samp_count), out_sha...  33.7 us
    pallas_call x1, Pallas kernels, fused_on_device(): pl.pallas_call(hand_out, out_shape=(jax.ShapeDtypeStruct((samples, LANES)...  1.57 us

profile of v2, /device:TPU:0, one launch (start us, length us, event | category | flops | bytes accessed | tf_op | source)
XLA Modules:
  0.0 35.9 jit_solution(16228181821196124484)
XLA Ops:
  0.6 33.7 %impute.1 = (bf16[512,128]{1,0:T(8,128)(2,1)}, f32[1,128]{1,0:T(1,128)}) custom-call(s32[512,1024]{1,0:T(8,128)} %tallies_hbm.1, s32[512,1024]{1,0:T(8,128)} %flags_hbm.1, s32[2048,1024]{1,0:T(8,128)} %strands_hbm.1, f32[1,512]{1,0:T(1,128)} %bitcast.4, f32[1,512]{1,0:T(1,128)} %bitcast.5, s32[1,512]{1,0:T(1,128)} %bitcast.6), custom_call_target="tpu_custom_call" | custom-call | tf_op jit(solution)/shard_map/impute/pallas_call | solution.py:508
  34.3 1.6 %hand_out.1 = (bf16[512,128]{1,0:T(8,128)(2,1)}, f32[1,128]{1,0:T(1,128)}) custom-call(bf16[512,128]{1,0:T(8,128)(2,1)} %get-tuple-element.6.dosage_in, f32[1,128]{1,0:T(1,128)} %get-tuple-element.7.zscore_in), custom_call_target="tpu_custom_call" | custom-call | tf_op jit(solution)/shard_map/hand_out/pallas_call | solution.py:570

commit v3 on v2

--- a/solution.py
+++ b/solution.py
@@ -86,7 +86,7 @@
 LANES = 128
 HAP_TILE = 256
 ROWS = 32
-VMEM_BYTES = 60 * 1024 * 1024
+VMEM_BYTES = 62 * 1024 * 1024
 
 
 def lane_copies(row):
@@ -356,11 +356,14 @@
 
     def allele_sums(chip):
         columns = pl.ds(pl.multiple_of(chip * 2 * LANES, 2 * LANES), 2 * LANES)
-        half = haps // 2
-        return jnp.dot(
-            weights_ref[:, :half], hap_ref[:half, columns], preferred_element_type=jnp.float32
-        ) + jnp.dot(
-            weights_ref[:, half:], hap_ref[half:, columns], preferred_element_type=jnp.float32
+        half = samples // 2
+        hap = hap_ref[:, columns]
+        return jnp.concatenate(
+            [
+                jnp.dot(weights_ref[k : k + half], hap, preferred_element_type=jnp.float32)
+                for k in (0, half)
+            ],
+            axis=0,
         )
 
     def hand_over(i):
@@ -491,11 +494,6 @@
         copy.wait_send()
 
 
-def hand_out(dosage_in, zscore_in, dosage_out, zscore_out):
-    dosage_out[...] = dosage_in[...]
-    zscore_out[...] = zscore_in[...]
-
-
 def fused_on_device(panel_count, samp_count, tallies, flags, strands, sharp, trait, cohort):
     samples, variants = tallies.shape
     haps = strands.shape[0]
@@ -508,8 +506,8 @@
     dosage, zscore = pl.pallas_call(
         functools.partial(fused, panel_count, samp_count),
         out_shape=(
-            jax.ShapeDtypeStruct((samples, LANES), bf16),
-            jax.ShapeDtypeStruct((1, LANES), f32),
+            pltpu.VMEM((samples, LANES), bf16),
+            pltpu.VMEM((1, LANES), f32),
         ),
         in_specs=[anywhere] * 3 + [local] * 3,
         out_specs=(local, local),
@@ -567,16 +565,6 @@
         trait.reshape(1, samples),
         cohort.reshape(1, samples),
     )
-    dosage, zscore = pl.pallas_call(
-        hand_out,
-        out_shape=(
-            jax.ShapeDtypeStruct((samples, LANES), bf16),
-            jax.ShapeDtypeStruct((1, LANES), f32),
-        ),
-        in_specs=[local, local],
-        out_specs=(local, local),
-        name="hand_out",
-    )(dosage, zscore)
     return dosage, zscore.reshape(LANES)
 
 

time: 36.1 us -> 34.5 us (0.956)
  Pallas kernels: 35.2 us -> 32.5 us
  local copies, waits for them, and re-layouts: 0 us -> 1.17 us
    pallas_call x1 -> x0, Pallas kernels: 1.57 us -> none  [fused_on_device(): pl.pallas_call(hand_out, out_shape=(jax.ShapeDtypeStruct((samples, LANES)...]
    unnamed x0 -> x2, local copies, waits for them, and re-layouts: none -> 1.17 us
    pallas_call x1, Pallas kernels: 33.7 us -> 32.5 us  [fused_on_device(): pl.pallas_call(functools.partial(fused, panel_count, samp_count), out_sha...]
where the time goes in v3:
time: 34.5 us; the launch traced here: 34.3 us
  Pallas kernels  32.5 us (94%)
  local copies, waits for them, and re-layouts  1.17 us (3%)
  between operations  0.64 us (2%)
    pallas_call x1, Pallas kernels, fused_on_device(): pl.pallas_call(functools.partial(fused, panel_count, samp_count), out_sha...  32.5 us
    unnamed x2, local copies, waits for them, and re-layouts  1.17 us

profile of v3, /device:TPU:0, one launch (start us, length us, event | category | flops | bytes accessed | tf_op | source)
XLA Modules:
  0.0 34.3 jit_solution(8475890090141910025)
XLA Ops:
  0.6 32.5 %impute.1 = (bf16[512,128]{1,0:T(8,128)(2,1)S(1)}, f32[1,128]{1,0:T(1,128)S(1)}) custom-call(s32[512,1024]{1,0:T(8,128)} %tallies_hbm.1, s32[512,1024]{1,0:T(8,128)} %flags_hbm.1, s32[2048,1024]{1,0:T(8,128)} %strands_hbm.1, f32[1,512]{1,0:T(1,128)} %bitcast.5, f32[1,512]{1,0:T(1,128)} %bitcast.6, s32[1,512]{1,0:T(1,128)} %bitcast.7), custom_call_target="tpu_custom_call" | custom-call | tf_op jit(solution)/shard_map/impute/pallas_call | solution.py:506
  33.2 0.7 %copy.10 = bf16[512,128]{1,0:T(8,128)(2,1)} copy(bf16[512,128]{1,0:T(8,128)(2,1)S(1)} %get-tuple-element.6) | data formatting | bytes 262144
  33.8 0.5 %copy.11 = f32[128]{0:T(128)} copy(f32[128]{0:T(128)S(1)} %bitcast.4) | data formatting | bytes 1024
